TPU v7x, 32 devices: a whole 2x2x4 slice. The times are simulated.
32 devices in a mesh: shard: 4 (over z), replica: 8 (over y, x, core).
Axes of the slice: x: 2, y: 2, z: 4, core: 2. Of those that a mesh axis runs over, the one named last changes fastest.
Arguments:
- atom_feats: bfloat16 [2048, 9, 128], P(('shard', 'replica')), may hold values from -6 to 6
- cotangent: bfloat16 [2048, 9, 128], P(('shard', 'replica')), may hold values from -6 to 6
- frames: bfloat16 [9, 9, 8192], P(None, None, ('shard', 'replica')), may hold values from -2 to 2
- radial: bfloat16 [8192, 128], P(('shard', 'replica')), may hold values from 0.19921875 to 2
- edge_source: int32 [8192], P(('shard', 'replica')), may hold values from 0 to 63
- edge_target: int32 [8192], P(('shard', 'replica')), may hold values from 0 to 63
- edge_valid: int32 [8192], P(('shard', 'replica')), may hold values 0 or 1
- atom_types: int32 [2048], P(('shard', 'replica')), may hold values from 0 to 99
- dataset: int32 [32], P(('shard', 'replica')), may hold values from 0 to 4
- type_table: float32 [100, 128], replicated, may hold values from -6 to 6
- dataset_table: float32 [5, 128], replicated, may hold values from -6 to 6
- router_weight: float32 [128, 28], replicated, may hold values from -1.5 to 1.5
- experts: bfloat16 [28, 384, 384], P(None, 'shard'), may hold values from -3 to 3
Outputs:
- updated: bfloat16 [2048, 9, 128], P(('shard', 'replica'))
- feats_grad: float32 [2048, 9, 128], P(('shard', 'replica'))
- expert_grad: float32 [28, 384, 384], P(None, 'shard')
Inputs may be any that keep to these rules, and one draw needn't show every extreme that they name: `edge_source`: indices of atoms within the edge's own system. `edge_target`: indices of atoms within the edge's own system.
All inputs are finite; a program needn't handle non-finite values. No bound on the sum of `edge_valid` on one device may be relied on, other than what follows from the above.
Results may differ from a plain program's by a relative error of at most 0.011.
Values may be sent and summed in bfloat16 or wider, within the bound.
A program may use at most 64 MiB of HBM per device.

v0:
```python
import math

import jax
import jax.numpy as jnp
from jax import lax
from jax.sharding import PartitionSpec as P


def system_mix(type_rows, dataset_one, type_table, dataset_table, router_weight):
    table_size = type_table.shape[0]
    onehot = (type_rows[:, None] == jnp.arange(table_size, dtype=jnp.int32)[None, :]).astype(
        jnp.float32
    )
    counts = jnp.sum(onehot, axis=0)
    embed = jnp.dot(counts, type_table, precision=lax.Precision.HIGHEST) / type_rows.shape[0]
    pick = (
        dataset_one[:, None] == jnp.arange(dataset_table.shape[0], dtype=jnp.int32)[None, :]
    ).astype(jnp.float32)
    embed = embed + jnp.dot(pick, dataset_table, precision=lax.Precision.HIGHEST)[0]
    soft = jax.nn.softplus(jnp.dot(embed, router_weight, precision=lax.Precision.HIGHEST))
    return soft / jnp.sum(soft)


def edge_layer(feats32, merged32, frames, radial, source, target, valid):
    atom_count, components, channels = feats32.shape
    edge_count = source.shape[0]
    top_degree = math.isqrt(components) - 1
    feats = feats32.astype(jnp.bfloat16)
    merged = merged32.astype(jnp.bfloat16)
    gathered = jnp.take(feats, source, axis=0)
    rotated = jnp.einsum(
        "ije,ejc->eic", frames.astype(jnp.float32), gathered.astype(jnp.float32)
    ).astype(jnp.bfloat16)
    zero_rows = [degree * degree + degree for degree in range(top_degree + 1)]
    zero_band = jnp.concatenate(
        [rotated[:, row : row + 1, :] for row in zero_rows], axis=1
    ).reshape(edge_count, -1)
    mixed_band = jnp.dot(zero_band, merged, preferred_element_type=jnp.float32).reshape(
        edge_count, top_degree + 1, channels
    )
    columns = []
    for column in range(components):
        if column in zero_rows:
            columns.append(mixed_band[:, zero_rows.index(column), :])
        else:
            columns.append(rotated[:, column, :].astype(jnp.float32))
    combined = jnp.stack(columns, axis=1)
    message = (combined * radial.astype(jnp.float32)[:, None, :]).astype(jnp.bfloat16)
    unrotated = jnp.einsum(
        "jie,ejc->eic", frames.astype(jnp.float32), message.astype(jnp.float32)
    ).astype(jnp.bfloat16)
    incidence = (
        (target[None, :] == jnp.arange(atom_count, dtype=jnp.int32)[:, None]) & (valid[None, :] > 0)
    ).astype(jnp.bfloat16)
    summed = jnp.dot(
        incidence, unrotated.reshape(edge_count, -1), preferred_element_type=jnp.float32
    )
    return feats32 + summed.reshape(atom_count, components, channels) * (atom_count / edge_count)


def add_system(total, pair):
    mix_row, rows = pair
    term = lax.optimization_barrier((mix_row[:, None, None] * rows[None]).astype(jnp.bfloat16))
    return (total + term.astype(jnp.float32), None)


def shards(
    atom_feats,
    cotangent,
    frames,
    radial,
    edge_source,
    edge_target,
    edge_valid,
    atom_types,
    dataset,
    type_table,
    dataset_table,
    router_weight,
    experts,
):
    group = lax.axis_size("shard")
    row_block = experts.shape[1]
    row_total = row_block * group
    mixture = system_mix(atom_types, dataset, type_table, dataset_table, router_weight)
    group_mixtures = lax.all_gather(mixture[None, :], "shard", axis=0, tiled=True)
    row_shares = jnp.einsum(
        "sk,krc->src", group_mixtures, experts.astype(jnp.float32), precision=lax.Precision.HIGHEST
    ).astype(jnp.bfloat16)
    merged = lax.all_to_all(row_shares, "shard", split_axis=0, concat_axis=1, tiled=True).reshape(
        row_total, -1
    )
    merged32 = lax.optimization_barrier(merged).astype(jnp.float32)

    def local(feats32, weight32):
        return edge_layer(feats32, weight32, frames, radial, edge_source, edge_target, edge_valid)

    result, pullback = jax.vjp(local, atom_feats.astype(jnp.float32), merged32)
    feats_grad, weight_grad = pullback(cotangent.astype(jnp.float32))
    back_mixtures = lax.all_gather(mixture[None, :], "shard", axis=0, tiled=True)
    received = lax.all_to_all(
        weight_grad.reshape(group, row_block, -1).astype(jnp.bfloat16),
        "shard",
        split_axis=0,
        concat_axis=0,
        tiled=True,
    ).astype(jnp.float32)
    start = jnp.zeros(experts.shape, jnp.float32)
    shard_sum, unused = lax.scan(add_system, start, (back_mixtures, received))
    expert_grad = lax.psum(shard_sum, "replica")
    return (result.astype(jnp.bfloat16), feats_grad, expert_grad)


def solution(mesh):
    in_specs = (
        P(("shard", "replica"), None, None),
        P(("shard", "replica"), None, None),
        P(None, None, ("shard", "replica")),
        P(("shard", "replica"), None),
        P(("shard", "replica")),
        P(("shard", "replica")),
        P(("shard", "replica")),
        P(("shard", "replica")),
        P(("shard", "replica")),
        P(),
        P(),
        P(),
        P(None, "shard", None),
    )
    out_specs = (
        P(("shard", "replica"), None, None),
        P(("shard", "replica"), None, None),
        P(None, "shard", None),
    )
    return jax.shard_map(shards, mesh=mesh, in_specs=in_specs, out_specs=out_specs, check_vma=False)
```

profile of v0, /device:TPU:0, one launch (start us, length us, event | category | flops | bytes accessed | tf_op | source)
XLA Modules:
  0.0 189.4 jit_solution(16895955329291108513)
XLA Ops:
  14.7 13.5 %all-reduce.11 = f32[112]{0:T(128)S(1)} all-reduce(f32[112]{0:T(128)S(1)} %divide_dynamic-update-slice_fusion), channel_id=2, replica_groups=mesh['shard'=4,'replica'=8] {'shard'}, use_global_device_ids=true, to_apply=%add.11 | all-reduce | flops 112 | bytes 896
  30.4 3.5 %all-to-all-start = ((bf16[4,96,384]{2,1,0:T(8,128)(2,1)}), bf16[4,96,384]{2,1,0:T(8,128)(2,1)S(1)}, u32[]{:S(2)}, u32[]{:S(2)}) async-start(bf16[4,96,384]{2,1,0:T(8,128)(2,1)} %copy.100), calls=%async_computation | async-start | bytes 589824 | tf_op jit(solution)/shard_map/all_to_all | solution.py:90
  38.2 1.7 copy.110
  39.9 1.9 copy.97
  41.8 3.8 %gather_fusion = bf16[256,9,128]{2,0,1:T(8,128)(2,1)} fusion(bf16[64,9,128]{2,0,1:T(8,128)(2,1)S(1)} %copy-done.1, s32[1024]{0:T(1024)} %pad_clamp_fusion), kind=kCustom, calls=%fused_computation | custom fusion | bytes 1180672 | tf_op jit(solution)/shard_map/jvp(jit(_take))/gather | solution.py:30
  50.0 1.8 copy.98
  51.8 2.6 %fusion.56 = (bf16[256,9,128]{2,1,0:T(8,128)(2,1)}, f32[256,9,128]{2,1,0:T(8,128)S(1)}) fusion(f32[256,128]{1,0:T(8,128)} %convert_element_type.132, bf16[256,9,128]{2,1,0:T(8,128)(2,1)} %copy.110, bf16[9,9,256]{1,0,2:T(8,128)(2,1)S(1)} %copy.97), kind=kOutput, calls=%fused_computation.91 | convolution fusion | flops 6488064 | bytes 2531840 | tf_op jit(solution)/shard_map/transpose(jvp(jie,ejc->eic))/dot_general | solution.py:49
  56.4 5.1 %all-to-all-start.1 = ((bf16[4,96,384]{2,1,0:T(8,128)(2,1)}), bf16[4,96,384]{2,1,0:T(8,128)(2,1)}, u32[]{:S(2)}, u32[]{:S(2)}) async-start(bf16[4,96,384]{2,1,0:T(8,128)(2,1)} %bitcast.24), calls=%async_computation.1 | async-start | bytes 589824 | tf_op jit(solution)/shard_map/all_to_all | solution.py:101
  62.1 1.9 %copy.106 = bf16[9,9,256]{0,1,2:T(8,128)(2,1)S(1)} copy(bf16[9,9,256]{2,1,0:T(8,128)(2,1)} %param.17) | data formatting | bytes 82944 | tf_op args[2]
  64.0 4.0 %fusion.52 = (bf16[256,1,128]{2,1,0:T(2,128)(2,1)}, bf16[256,1,128]{2,1,0:T(2,128)(2,1)}, bf16[256,1,128]{2,1,0:T(2,128)(2,1)}, bf16[256,1,128]{2,1,0:T(2,128)(2...) fusion(bf16[256,9,128]{2,1,0:T(8,128)(2,1)} %get-tuple-element.74), kind=kLoop, calls=%fused_computation.87 | loop fusion | bytes 786432 | tf_op jit(solution)/shard_map/transpose(jvp())/unstack | solution.py:47
  69.0 1.8 convert_element_type.147
  70.8 25.5 %while.11 = (s32[]{:T(128)}, f32[28,96,384]{2,1,0:T(8,128)}, f32[4,28]{1,0:T(4,128)}, f32[4,96,384]{2,1,0:T(8,128)}, s32[]{:T(128)}, /*index=5*/s32[]{:T(128)}) while((s32[]{:T(128)}, f32[28,96,384]{2,1,0:T(8,128)}, f32[4,28]{1,0:T(4,128)}, f32[4,96,384]{2,1,0:T(8,128)}, s32[]{:T(128)}, /*index=5*/s32[]{:T(128)}) %tuple.48), condition=%wide.region_4.5_spmd.clone, body=%wide.region_3.4_spmd.clone.sunk | while | flops 5160963 | bytes 12829103 | solution.py:109
  72.9 2.7 %select_add_fusion.2 = f32[28,96,384]{2,1,0:T(8,128)} fusion(f32[28,96,384]{2,1,0:T(8,128)} %get-tuple-element.108, bf16[28,96,384]{2,1,0:T(8,128)(2,1)S(1)} %multiply_convert_fusion.4, pred[]{:T(512)S(6)} %compare.14), kind=kLoop, calls=%fused_computation.2.clone.1 | loop fusion | flops 3096576 | bytes 10321921 | tf_op jit(solution)/shard_map/while/body/eval_jaxpr/add | solution.py:64
  77.6 4.8 %select_add_fusion.2 = f32[28,96,384]{2,1,0:T(8,128)} fusion(f32[28,96,384]{2,1,0:T(8,128)} %get-tuple-element.108, bf16[28,96,384]{2,1,0:T(8,128)(2,1)S(1)} %multiply_convert_fusion.4, pred[]{:T(512)S(6)} %compare.14), kind=kLoop, calls=%fused_computation.2.clone.1 | loop fusion | flops 3096576 | bytes 10321921 | tf_op jit(solution)/shard_map/while/body/eval_jaxpr/add | solution.py:64
  84.5 4.8 %select_add_fusion.2 = f32[28,96,384]{2,1,0:T(8,128)} fusion(f32[28,96,384]{2,1,0:T(8,128)} %get-tuple-element.108, bf16[28,96,384]{2,1,0:T(8,128)(2,1)S(1)} %multiply_convert_fusion.4, pred[]{:T(512)S(6)} %compare.14), kind=kLoop, calls=%fused_computation.2.clone.1 | loop fusion | flops 3096576 | bytes 10321921 | tf_op jit(solution)/shard_map/while/body/eval_jaxpr/add | solution.py:64
  91.4 4.8 %select_add_fusion.2 = f32[28,96,384]{2,1,0:T(8,128)} fusion(f32[28,96,384]{2,1,0:T(8,128)} %get-tuple-element.108, bf16[28,96,384]{2,1,0:T(8,128)(2,1)S(1)} %multiply_convert_fusion.4, pred[]{:T(512)S(6)} %compare.14), kind=kLoop, calls=%fused_computation.2.clone.1 | loop fusion | flops 3096576 | bytes 10321921 | tf_op jit(solution)/shard_map/while/body/eval_jaxpr/add | solution.py:64
  98.5 7.0 %stack.2 = f32[256,9,128]{2,1,0:T(8,128)} concatenate(f32[256,1,128]{2,1,0:T(1,128)} %bitcast.98, f32[256,1,128]{2,1,0:T(1,128)} %get-tuple-element.62, f32[256,1,128]{2,1,0:T(1,128)} %bitcast.97, f32[256,1,128]{2,1,0:T(1,128)} %get-tuple-element.61, f32[256,1,128]{2,1,0:T(1,128)} %get-tuple-element.60, f32[256,1,128]{2,1,0:T(1,128)} %get-tuple-element.59, ...), dimensions={1} | concatenate | bytes 2359296 | tf_op jit(solution)/shard_map/jvp()/stack | solution.py:47
  105.4 3.0 %fusion.3 = bf16[256,9,128]{2,1,0:T(8,128)(2,1)} fusion(bf16[9,9,256]{0,1,2:T(8,128)(2,1)S(1)} %copy.106, f32[256,9,128]{2,1,0:T(8,128)} %stack.2, f32[256,128]{1,0:T(8,128)} %convert_element_type.132), kind=kOutput, calls=%fused_computation.16 | convolution fusion | flops 6193152 | bytes 1942016 | tf_op jit(solution)/shard_map/jvp(jie,ejc->eic)/dot_general | solution.py:49
  108.5 2.4 %copy.107 = bf16[256,9,128]{0,2,1:T(8,128)(2,1)} copy(bf16[256,9,128]{2,1,0:T(8,128)(2,1)} %fusion.3) | data formatting | bytes 1179648 | tf_op jit(solution)/shard_map/jvp()/convert_element_type | solution.py:51
  113.3 3.9 %fusion.4 = bf16[256,9,128]{2,1,0:T(8,128)(2,1)S(1)} fusion(bf16[9,9,256]{0,1,2:T(8,128)(2,1)} %copy-done.2, bf16[256,1,128]{2,1,0:T(2,128)(2,1)} %copy.126, bf16[256,1,128]{2,1,0:T(2,128)(2,1)S(1)} %copy.125, bf16[256,1,128]{2,1,0:T(2,128)(2,1)S(1)} %copy.124, bf16[256,1,128]{2,1,0:T(2,128)(2,1)} %get-tuple-element.52, ...), kind=kOutput, calls=%fused_computation.17 | convolution fusion | flops 10911744 | bytes 1221120 | tf_op jit(solution)/shard_map/transpose(jvp(ije,ejc->eic))/dot_general | solution.py:31
  117.3 9.3 %scatter_fusion = bf16[64,9,128]{2,1,0:T(8,128)(2,1)S(1)} fusion(bf16[64,9,128]{2,1,0:T(8,128)(2,1)S(1)} %broadcast_in_dim.24, s32[256]{0:T(256)S(1)} %copy-done.8, bf16[256,9,128]{2,1,0:T(8,128)(2,1)S(1)} %fusion.4), kind=kCustom, calls=%fused_computation.1 | custom fusion | flops 294912 | bytes 1770496 | tf_op jit(solution)/shard_map/transpose(jvp(jit(_take)))/scatter-add | solution.py:30
  128.3 2.1 %fusion.9 = bf16[64,9,128]{2,0,1:T(8,128)(2,1)} fusion(bf16[256,9,128]{0,2,1:T(8,128)(2,1)} %copy.107, bf16[64,9,128]{2,0,1:T(8,128)(2,1)S(1)} %copy-done.1, s32[256]{0:T(256)S(1)} %copy-done.10, pred[256]{0:T(512)(128)(4,1)S(1)} %copy-done.12), kind=kOutput, calls=%fused_computation.23 | convolution fusion | flops 38076416 | bytes 886016 | tf_op jit(solution)/shard_map/jvp()/dot_general | solution.py:55
  130.4 47.8 %all-reduce.14.cloned.1.call-done = f32[28,96,384]{2,1,0:T(8,128)} async-done(((f32[28,96,384]{2,1,0:T(8,128)}), f32[28,96,384]{2,1,0:T(8,128)}) %all-reduce.14.cloned.1.call-update) | async-done | bytes 4128784 | tf_op jit(solution)/shard_map/psum | solution.py:110
  178.2 4.4 %copy.149 = f32[28,96,384]{2,1,0:T(8,128)} copy(f32[28,96,384]{2,1,0:T(8,128)} %all-reduce.14.cloned.1.call-done) | data formatting | bytes 8257536
  (90 shorter events, 35.0 us)
Async XLA Ops:
  7.2 21.1 %copy-start = (bf16[28,96,384]{2,1,0:T(8,128)(2,1)S(1)}, bf16[28,96,384]{2,1,0:T(8,128)(2,1)}, u32[]{:S(2)}) copy-start(bf16[28,96,384]{2,1,0:T(8,128)(2,1)} %param.27) | copy-start | bytes 6193156
  7.2 26.7 %copy-start.15 = (s32[256]{0:T(256)S(1)}, s32[256]{0:T(256)}, u32[]{:S(2)}) copy-start(s32[256]{0:T(256)} %param.19) | copy-start | bytes 3076
  7.2 27.1 %copy-start.17 = (s32[256]{0:T(256)S(1)}, s32[256]{0:T(256)}, u32[]{:S(2)}) copy-start(s32[256]{0:T(256)} %param.21) | copy-start | bytes 3076
  7.2 27.8 %copy-start.6 = (bf16[256,128]{1,0:T(8,128)(2,1)S(1)}, bf16[256,128]{1,0:T(8,128)(2,1)}, u32[]{:S(2)}) copy-start(bf16[256,128]{1,0:T(8,128)(2,1)} %param.18) | copy-start | bytes 196612
  7.2 28.4 %copy-start.9 = (s32[256]{0:T(256)S(1)}, s32[256]{0:T(256)}, u32[]{:S(2)}) copy-start(s32[256]{0:T(256)} %param.20) | copy-start | bytes 3076
  7.2 28.4 %copy-start.5 = (bf16[64,9,128]{2,0,1:T(8,128)(2,1)S(1)}, bf16[64,9,128]{2,0,1:T(8,128)(2,1)}, u32[]{:S(2)}) copy-start(bf16[64,9,128]{2,0,1:T(8,128)(2,1)} %param.16) | copy-start | bytes 442372
  28.2 6.2 %copy-start.13 = (f32[112]{0:T(128)}, f32[112]{0:T(128)S(1)}, u32[]{:S(2)}) copy-start(f32[112]{0:T(128)S(1)} %all-reduce.11) | copy-start | bytes 1348
  30.4 26.0 %all-to-all-start = ((bf16[4,96,384]{2,1,0:T(8,128)(2,1)}), bf16[4,96,384]{2,1,0:T(8,128)(2,1)S(1)}, u32[]{:S(2)}, u32[]{:S(2)}) async-start(bf16[4,96,384]{2,1,0:T(8,128)(2,1)} %copy.100), calls=%async_computation | async-start | bytes 589824 | tf_op jit(solution)/shard_map/all_to_all | solution.py:90
  34.3 1.3 copy-start.7
  34.4 1.3 copy-start.11
  36.8 4.9 %copy-start.1 = (bf16[64,9,128]{2,0,1:T(8,128)(2,1)S(1)}, bf16[64,9,128]{2,0,1:T(8,128)(2,1)}, u32[]{:S(2)}) copy-start(bf16[64,9,128]{2,0,1:T(8,128)(2,1)} %param.15) | copy-start | bytes 442372
  51.8 2.9 %copy-start.16 = (pred[3]{0:T(512)(128)(4,1)S(1)}, pred[3]{0:T(512)(128)(4,1)}, u32[]{:S(2)}) copy-start(pred[3]{0:T(512)(128)(4,1)} %constant.42.clone.1) | copy-start | bytes 13
  54.5 0.9 copy-start.3
  54.5 7.0 %copy-start.14 = (f32[112]{0:T(128)S(1)}, f32[112]{0:T(128)}, u32[]{:S(2)}) copy-start(f32[112]{0:T(128)} %copy-done.13) | copy-start | bytes 1348
  55.2 6.2 %copy-start.4 = (bf16[256,3,128]{0,2,1:T(8,128)(2,1)}, bf16[256,3,128]{0,2,1:T(8,128)(2,1)S(1)}, u32[]{:S(2)}) copy-start(bf16[256,3,128]{0,2,1:T(8,128)(2,1)S(1)} %copy.112) | copy-start | bytes 589828
  56.4 12.6 %all-to-all-start.1 = ((bf16[4,96,384]{2,1,0:T(8,128)(2,1)}), bf16[4,96,384]{2,1,0:T(8,128)(2,1)}, u32[]{:S(2)}, u32[]{:S(2)}) async-start(bf16[4,96,384]{2,1,0:T(8,128)(2,1)} %bitcast.24), calls=%async_computation.1 | async-start | bytes 589824 | tf_op jit(solution)/shard_map/all_to_all | solution.py:101
  61.4 116.7 %all-reduce.14.cloned.1.call-start = ((), (), s32[]{:S(2)}) async-start(), calls=%async_computation.2 | async-start | bytes 8257536 | tf_op jit(solution)/shard_map/psum | solution.py:110
  64.0 41.4 %copy-start.2 = (bf16[9,9,256]{0,1,2:T(8,128)(2,1)}, bf16[9,9,256]{0,1,2:T(8,128)(2,1)S(1)}, u32[]{:S(2)}) copy-start(bf16[9,9,256]{0,1,2:T(8,128)(2,1)S(1)} %copy.106) | copy-start | bytes 124420
  113.3 4.0 %copy-start.8 = (s32[256]{0:T(256)S(1)}, s32[256]{0:T(256)}, u32[]{:S(2)}) copy-start(s32[256]{0:T(256)} %copy-done.7) | copy-start | bytes 3076
  117.3 11.0 %copy-start.10 = (s32[256]{0:T(256)S(1)}, s32[256]{0:T(256)}, u32[]{:S(2)}) copy-start(s32[256]{0:T(256)} %param.20) | copy-start | bytes 3076
  117.3 11.0 %copy-start.12 = (pred[256]{0:T(512)(128)(4,1)S(1)}, pred[256]{0:T(512)(128)(4,1)}, u32[]{:S(2)}) copy-start(pred[256]{0:T(512)(128)(4,1)} %copy-done.11) | copy-start | bytes 772
Sparse Core Ops, SparseCore 0:
  96.4 81.6 all-reduce.13
where the time goes:
time: 191 us; the launch traced here: 189 us
  waiting for transfers between devices  47.8 us (25%)
  local copies, waits for them, and re-layouts  42.7 us (22%)
  other arithmetic  39.5 us (21%)
  matrix products  21.7 us (11%)
  between operations  15.8 us (8%)
  blocking collectives  13.5 us (7%)
  starting transfers between devices  8.51 us (4%)
    psum x1, waiting for transfers between devices, shards(): expert_grad = lax.psum(shard_sum, 'replica')  47.8 us
    add x4, other arithmetic, add_system(): return (total + term.astype(jnp.float32), None)  17.2 us
    unnamed x1, blocking collectives  13.5 us
    another operation x3, local copies, waits for them, and re-layouts, edge_layer(): combined = jnp.stack(columns, axis=1)  11.2 us
    unnamed x44, local copies, waits for them, and re-layouts  10.7 us
    scatter-add x1, other arithmetic, edge_layer(): gathered = jnp.take(feats, source, axis=0)  9.31 us
    mul x8, local copies, waits for them, and re-layouts, add_system(): mix_row[:, None, None] * rows[None]  6.35 us
    dot_general x2, matrix products, edge_layer(): jnp.einsum('jie,ejc->eic', frames.astype(jnp.float32), message.astype(jnp...  5.67 us
  transfers between devices with their start and end apart: 3, of which 1 were waited for; matrix products, arithmetic and copies ran while one was open for 34% of the time, Pallas kernels for 0%

commit v1 on v0

v1 whole, which is shorter than its diff:
```python
import functools
import math

import jax
import jax.numpy as jnp
from jax import lax
from jax.experimental import pallas as pl
from jax.experimental.pallas import tpu as pltpu
from jax.sharding import PartitionSpec as P

MESH = pl.DeviceIdType.MESH
VMEM = pltpu.VMEM
F32 = jnp.float32
BF16 = jnp.bfloat16
ROWS = 16
NN = (((1,), (0,)), ((), ()))
NT = (((1,), (1,)), ((), ()))
TN = (((0,), (0,)), ((), ()))


def dot(a, b, dims=NN):
    return lax.dot_general(a, b, dims, preferred_element_type=F32)


def spread(mix, systems, experts, by_expert):
    mix = mix.astype(BF16)
    shape = (experts * ROWS, mix.shape[1])
    pick = (lax.broadcasted_iota(jnp.int32, shape, 0) // ROWS == lax.broadcasted_iota(jnp.int32, shape, 1)).astype(BF16)
    shape = (systems * ROWS, systems)
    own = (lax.broadcasted_iota(jnp.int32, shape, 0) // ROWS == lax.broadcasted_iota(jnp.int32, shape, 1)).astype(BF16)
    if by_expert:
        wide = dot(dot(pick, mix, NT).astype(BF16), own, NT)
    else:
        wide = dot(dot(own, mix).astype(BF16), pick, NT)
    row = lax.broadcasted_iota(jnp.int32, wide.shape, 0) % ROWS
    col = lax.broadcasted_iota(jnp.int32, wide.shape, 1) % ROWS
    return jnp.where(row == col, wide, 0.0).astype(BF16)


def rotate(frame_scr, first, second, out_fn, transposed, channels):
    comps = first.shape[0]

    def step(t, carry):
        at = pl.ds(pl.multiple_of(t * ROWS, ROWS), ROWS)
        edges = first.shape[2]
        one = [first[j, at, :].astype(F32).reshape(2, ROWS // 2, edges) for j in range(comps)]
        two = [second[j, at, :].astype(F32).reshape(2, ROWS // 2, edges) for j in range(comps)]
        for i in range(comps):
            a = b = None
            for j in range(comps):
                f = frame_scr[(j * comps + i) if transposed else (i * comps + j)][None]
                a = f * one[j] if a is None else a + f * one[j]
                b = f * two[j] if b is None else b + f * two[j]
            out_fn(i, at, a.reshape(ROWS, edges), b.reshape(ROWS, edges))
        return carry

    lax.fori_loop(0, channels // ROWS, step, 0)


def fill_frames(frames, frame_scr):
    comps = frames.shape[0]
    for i in range(comps):
        rows = frames[i].astype(F32)
        for j in range(comps):
            frame_scr[i * comps + j] = jnp.broadcast_to(rows[j : j + 1, :], frame_scr.shape[1:])


def hits(index, atoms):
    return lax.broadcasted_iota(jnp.int32, (atoms, index.shape[1]), 0) == index


def before_kernel(
    feats, cot, frames, radial, source, target, valid, types, dataset, type_table, dataset_table, router,
    mix, weight_grad, rotated, dcomb, spread_scr, gat_scr, dun_scr, frame_scr, rad_scr, router_scr,
):
    atoms, comps, channels = feats.shape
    zero_rows = [d * d + d for d in range(math.isqrt(comps))]
    n_types, n_exp = type_table.shape[0], router.shape[1]
    onehot = (lax.broadcasted_iota(jnp.int32, (n_types, atoms), 0) == types[...]).astype(F32)
    counts = jnp.sum(onehot, axis=1, keepdims=True)
    embed = jnp.sum(counts * type_table[...], axis=0, keepdims=True) / atoms
    n_sets = dataset_table.shape[0]
    pick = (lax.broadcasted_iota(jnp.int32, (n_sets, 1), 0) == dataset[...]).astype(F32)
    embed = embed + jnp.sum(pick * dataset_table[...], axis=0, keepdims=True)
    router_scr[...] = jnp.zeros_like(router_scr)
    router_scr[:, :n_exp] = router[...]
    logits = lax.dot_general(embed, router_scr[...], NN, precision=lax.Precision.HIGHEST, preferred_element_type=F32)
    soft = jnp.maximum(logits, 0.0) + jnp.log1p(jnp.exp(-jnp.abs(logits)))
    soft = jnp.where(lax.broadcasted_iota(jnp.int32, soft.shape, 1) < n_exp, soft, 0.0)
    mix[...] = soft / jnp.sum(soft, axis=1, keepdims=True)

    fill_frames(frames, frame_scr)
    rad_scr[...] = radial[...].astype(F32).T
    src = hits(source[...], atoms).astype(BF16)
    tgt = (hits(target[...], atoms) & (valid[...] > 0)).astype(BF16)
    scale = atoms / source.shape[1]
    spread_scr[...] = feats[...].astype(F32)
    for j in range(comps):
        gat_scr[j] = dot(spread_scr[:, j, :].astype(BF16), src, TN).astype(BF16)
    spread_scr[...] = cot[...].astype(F32) * scale
    for j in range(comps):
        dun_scr[j] = dot(spread_scr[:, j, :].astype(BF16), tgt, TN).astype(BF16)

    def out(i, at, a, b):
        rotated[i, at, :] = a.astype(BF16)
        dcomb[i, at, :] = (b.astype(BF16).astype(F32) * rad_scr[at, :]).astype(BF16)

    rotate(frame_scr, gat_scr, dun_scr, out, False, channels)
    for p, i in enumerate(zero_rows):
        for q, j in enumerate(zero_rows):
            weight_grad[p * channels : (p + 1) * channels, q * channels : (q + 1) * channels] = dot(
                rotated[i], dcomb[j], NT
            ).astype(BF16)


def exchange_kernel(
    group, replicas, mix, weight_grad, experts,
    mix_all, rows_all, merged, mix_group, shares, experts_scr, kron_scr,
    local_sem, mix_send, mix_recv, mixall_send, mixall_recv, wg_send, own_send, rows_recv, merged_send, merged_recv,
):
    z, r = lax.axis_index("shard"), lax.axis_index("replica")
    n_exp, block, width = experts.shape
    peers = [lax.rem(z + o, group) for o in range(group)]
    core = lax.rem(r, 2)
    bits = max(replicas.bit_length() - 1, 1)
    dims = [1 << b for b in range(1, bits)]

    def flip(index, bit):
        return index + bit * (1 - 2 * lax.rem(index // bit, 2))

    order = [jnp.where(core == 0, a, b) for a, b in zip(dims, dims[::-1])]
    sibling = flip(r, 1)

    fetch = pltpu.make_async_copy(experts, experts_scr, local_sem.at[0])
    fetch.start()
    keep = pltpu.make_async_copy(
        weight_grad.at[pl.ds(pl.multiple_of(z * block, ROWS), block)], rows_all.at[r, z], local_sem.at[1]
    )
    keep.start()

    barrier = pltpu.get_barrier_semaphore()
    for p in peers[1:]:
        pl.semaphore_signal(barrier, inc=1, device_id=(p, r), device_id_type=MESH)
    for o in range(1, replicas):
        pl.semaphore_signal(barrier, inc=1, device_id=(z, lax.rem(r + o, replicas)), device_id_type=MESH)
    mix_group[z] = mix[...]
    pl.semaphore_wait(barrier, group - 1 + replicas - 1)

    def remote(src, dst, send, recv, device):
        return pltpu.make_async_remote_copy(
            src_ref=src, dst_ref=dst, send_sem=send, recv_sem=recv, device_id=device, device_id_type=MESH
        )

    mix_copies = [
        remote(mix, mix_group.at[z], mix_send.at[n], mix_recv.at[z], (p, r)) for n, p in enumerate(peers[1:])
    ]
    for copy in mix_copies:
        copy.start()
    wg_copies = [
        remote(
            weight_grad.at[pl.ds(pl.multiple_of(p * block, ROWS), block)],
            rows_all.at[r, z], wg_send.at[n], rows_recv.at[r, z], (p, r),
        )
        for n, p in enumerate(peers[1:])
    ]
    for copy in wg_copies:
        copy.start()

    sent = [0]
    pending = []

    def forward(n, mask):
        who = r
        top = -1
        for k in range(len(dims)):
            if mask >> k & 1:
                who = flip(who, order[k])
                top = k
        slot = rows_all.at[who, peers[n]]
        if mask or n:
            remote(slot, slot, own_send.at[0], rows_recv.at[who, peers[n]], (z, r)).wait_recv()
        goals = [flip(r, order[k]) for k in range(top + 1, len(dims))] + [sibling]
        for goal in goals if replicas > 1 else []:
            copy = remote(slot, slot, own_send.at[sent[0]], rows_recv.at[who, peers[n]], (z, goal))
            copy.start()
            pending.append(copy)
            sent[0] += 1

    keep.wait()
    forward(0, 0)

    for n, p in enumerate(peers[1:]):
        remote(mix, mix_group.at[p], mix_send.at[0], mix_recv.at[p], (z, r)).wait_recv()
    mixall_copies = []
    for o in range(1, replicas):
        copy = remote(
            mix_group, mix_all.at[r], mixall_send.at[o - 1], mixall_recv.at[r], (z, lax.rem(r + o, replicas))
        )
        copy.start()
        mixall_copies.append(copy)
    mix_all[r] = mix_group[...]
    kron_scr[...] = spread(mix_group[...].reshape(group, mix.shape[1]), group, n_exp, False)
    fetch.wait()
    for t in range(block // ROWS):
        at = slice(t * ROWS, (t + 1) * ROWS)
        shares[:, at, :] = (
            dot(kron_scr[...], experts_scr[:, at, :].reshape(n_exp * ROWS, width)).astype(BF16).reshape(group, ROWS, width)
        )
    own_rows = pl.ds(pl.multiple_of(z * block, ROWS), block)
    merged_copies = [
        remote(shares.at[p], merged.at[own_rows], merged_send.at[n], merged_recv.at[z], (p, r))
        for n, p in enumerate(peers[1:])
    ]
    for copy in merged_copies:
        copy.start()
    merged[own_rows, :] = shares[z]

    masks = 1 << len(dims)
    for n in range(1, group):
        forward(n, 0)
        for mask in range(1, masks):
            forward(n - 1, mask)
    for mask in range(1, masks):
        forward(group - 1, mask)
    if replicas > 1:
        for n in range(group):
            for mask in range(masks):
                who = sibling
                for k in range(len(dims)):
                    if mask >> k & 1:
                        who = flip(who, dims[k])
                slot = rows_all.at[who, peers[n]]
                remote(slot, slot, own_send.at[0], rows_recv.at[who, peers[n]], (z, r)).wait_recv()
    for o in range(1, replicas):
        who = lax.rem(r + o, replicas)
        remote(mix_group, mix_all.at[who], mixall_send.at[0], mixall_recv.at[who], (z, r)).wait_recv()
    for p in peers[1:]:
        rows = pl.ds(pl.multiple_of(p * block, ROWS), block)
        remote(shares.at[p], merged.at[rows], merged_send.at[0], merged_recv.at[p], (z, r)).wait_recv()
    for copy in mix_copies + wg_copies + mixall_copies + merged_copies + pending:
        copy.wait_send()


def after_kernel(
    feats, cot, frames, radial, source, target, valid, rotated, dcomb, merged, mix_all, rows_all,
    updated, feats_grad, expert_grad,
    spread_scr, msg_scr, drot_scr, un_scr, dgat_scr, frame_scr, rad_scr, kron_scr, out_scr, out_sem,
):
    atoms, comps, channels = feats.shape
    zero_rows = [d * d + d for d in range(math.isqrt(comps))]
    systems, block, width = rows_all.shape
    n_exp = expert_grad.shape[0]
    piece = min(systems, 32)
    tiles = block // ROWS
    copies = []
    for part in range(systems // piece):
        at = slice(part * piece, (part + 1) * piece)
        kron_scr[part] = spread(mix_all[at].reshape(piece, mix_all.shape[2]), piece, n_exp, True)
    for t in range(tiles):
        if t >= 2:
            copies[t - 2].wait()
        rows = slice(t * ROWS, (t + 1) * ROWS)
        total = None
        for part in range(systems // piece):
            at = slice(part * piece, (part + 1) * piece)
            term = dot(kron_scr[part], rows_all[at, rows, :].reshape(piece * ROWS, width))
            total = term if total is None else total + term
        out_scr[t % 2] = total.reshape(n_exp, ROWS, width)
        copy = pltpu.make_async_copy(out_scr.at[t % 2], expert_grad.at[:, rows, :], out_sem.at[t % 2])
        copy.start()
        copies.append(copy)

    fill_frames(frames, frame_scr)
    rad_scr[...] = radial[...].astype(F32).T
    band = len(zero_rows) * channels
    zero_band = jnp.concatenate([rotated[i] for i in zero_rows], axis=0)
    dmixed = jnp.concatenate([dcomb[i] for i in zero_rows], axis=0)
    mixed = dot(merged[...], zero_band, TN)
    dzero = dot(merged[...], dmixed).astype(BF16)
    rad = rad_scr[...]
    for i in range(comps):
        if i in zero_rows:
            at = slice(zero_rows.index(i) * channels, (zero_rows.index(i) + 1) * channels)
            msg_scr[i] = (mixed[at] * rad).astype(BF16)
            drot_scr[i] = dzero[at]
        else:
            msg_scr[i] = (rotated[i].astype(F32) * rad).astype(BF16)
            drot_scr[i] = dcomb[i]

    def out(i, at, a, b):
        un_scr[i, at, :] = a.astype(BF16)
        dgat_scr[i, at, :] = b.astype(BF16)

    rotate(frame_scr, msg_scr, drot_scr, out, True, channels)
    src = hits(source[...], atoms).astype(BF16)
    tgt = (hits(target[...], atoms) & (valid[...] > 0)).astype(BF16)
    scale = atoms / source.shape[1]
    for i in range(comps):
        spread_scr[:, i, :] = dot(tgt, un_scr[i], NT) * scale
        feats_grad[:, i, :] = dot(src, dgat_scr[i], NT).astype(BF16).astype(F32)
    updated[...] = (feats[...].astype(F32) + spread_scr[...]).astype(BF16)
    feats_grad[...] = feats_grad[...] + cot[...].astype(F32)
    for copy in copies[-2:]:
        copy.wait()


def call(kernel, out_shape, scratch, ins, outs=None, collective=None):
    vmem = pl.BlockSpec(memory_space=VMEM)
    anywhere = pl.BlockSpec(memory_space=pl.ANY)
    extra = {} if collective is None else {"collective_id": collective, "has_side_effects": True}
    return pl.pallas_call(
        kernel,
        out_shape=out_shape,
        in_specs=[anywhere if hbm else vmem for hbm in ins],
        out_specs=[anywhere if hbm else vmem for hbm in (outs or [0] * len(out_shape))],
        scratch_shapes=scratch,
        compiler_params=pltpu.CompilerParams(vmem_limit_bytes=56 << 20, **extra),
    )


def shards(
    atom_feats, cotangent, frames, radial, edge_source, edge_target, edge_valid, atom_types, dataset,
    type_table, dataset_table, router_weight, experts,
):
    group, replicas = lax.axis_size("shard"), lax.axis_size("replica")
    atoms, comps, channels = atom_feats.shape
    edges = edge_source.shape[0]
    n_exp, block, width = experts.shape
    source, target, valid = (a.reshape(1, edges) for a in (edge_source, edge_target, edge_valid))
    shape = jax.ShapeDtypeStruct
    stack = (comps, channels, edges)
    lanes = 128
    frame_scr = VMEM((comps * comps, ROWS // 2, edges), F32)
    rad_scr = VMEM((channels, edges), F32)
    mix, weight_grad, rotated, dcomb = call(
        before_kernel,
        [shape((1, lanes), F32), shape((block * group, width), BF16), shape(stack, BF16), shape(stack, BF16)],
        [
            VMEM((atoms, comps, channels), F32), VMEM(stack, BF16), VMEM(stack, BF16), frame_scr, rad_scr,
            VMEM((router_weight.shape[0], lanes), F32),
        ],
        [0] * 12,
    )(
        atom_feats, cotangent, frames, radial, source, target, valid, atom_types.reshape(1, atoms),
        dataset.reshape(1, 1), type_table, dataset_table, router_weight,
    )
    sem = pltpu.SemaphoreType.DMA
    few = max(group - 1, 1)
    many = max(replicas - 1, 1)
    mix_all, rows_all, merged = call(
        functools.partial(exchange_kernel, group, replicas),
        [
            shape((replicas, group, 1, lanes), F32),
            shape((replicas, group, block, width), BF16),
            shape((block * group, width), BF16),
        ],
        [
            VMEM((group, 1, lanes), F32), VMEM((group, block, width), BF16), VMEM(experts.shape, BF16),
            VMEM((group * ROWS, n_exp * ROWS), BF16),
            sem((2,)), sem((few,)), sem((group,)), sem((many,)), sem((replicas,)), sem((few,)),
            sem((many * group,)), sem((replicas, group)), sem((few,)), sem((group,)),
        ],
        [0, 0, 1],
        collective=0,
    )(mix, weight_grad, experts)
    systems = group * replicas
    piece = min(systems, 32)
    updated, feats_grad, expert_grad = call(
        after_kernel,
        [shape(atom_feats.shape, BF16), shape(atom_feats.shape, F32), shape(experts.shape, F32)],
        [
            VMEM((atoms, comps, channels), F32), VMEM(stack, BF16), VMEM(stack, BF16), VMEM(stack, BF16),
            VMEM(stack, BF16), frame_scr, rad_scr, VMEM((systems // piece, n_exp * ROWS, piece * ROWS), BF16),
            VMEM((2, n_exp, ROWS, width), F32), sem((2,)),
        ],
        [0] * 12,
        [0, 0, 1],
    )(
        atom_feats, cotangent, frames, radial, source, target, valid, rotated, dcomb, merged,
        mix_all.reshape(systems, 1, lanes), rows_all.reshape(systems, block, width),
    )
    return (updated, feats_grad, expert_grad)


def solution(mesh):
    both = ("shard", "replica")
    in_specs = (
        P(both, None, None), P(both, None, None), P(None, None, both), P(both, None),
        P(both), P(both), P(both), P(both), P(both), P(), P(), P(), P(None, "shard", None),
    )
    out_specs = (P(both, None, None), P(both, None, None), P(None, "shard", None))
    return jax.shard_map(shards, mesh=mesh, in_specs=in_specs, out_specs=out_specs, check_vma=False)
```

time: 191 us -> 60.6 us (0.32)
  the two profiles are of different devices: /device:TPU:0 before, /device:TPU:9 now
where the time goes in v1:
time: 60.6 us; the launch traced here: 60.3 us
  Pallas kernels  50.6 us (83%)
  local copies, waits for them, and re-layouts  8.4 us (14%)
  between operations  1.3 us (2%)
    pallas_call x1, Pallas kernels, shards(): call(functools.partial(exchange_kernel, group, replicas), [shape((replica...  35.8 us
    pallas_call x1, Pallas kernels, shards(): call(after_kernel, [shape(atom_feats.shape, BF16), shape(atom_feats.shape...  9.5 us
    pallas_call x1, Pallas kernels, shards(): call(before_kernel, [shape((1, lanes), F32), shape((block * group, width)...  5.32 us
    unnamed x3, local copies, waits for them, and re-layouts  4.89 us
    pallas_call x2, local copies, waits for them, and re-layouts, shards(): call(after_kernel, [shape(atom_feats.shape, BF16), shape(atom_feats.shape...  3.5 us

profile of v1, /device:TPU:9, one launch (start us, length us, event | category | flops | bytes accessed | tf_op | source)
XLA Modules:
  0.0 60.3 jit_solution(13176223092676164398)
XLA Ops:
  1.3 1.4 %copy.18.router = f32[128,28]{1,0:T(8,128)} copy(f32[128,28]{0,1:T(8,128)} %param.24) | data formatting | bytes 28672 | tf_op args[11]
  2.7 1.7 %copy.19.feats = bf16[64,9,128]{2,1,0:T(8,128)(2,1)} copy(bf16[64,9,128]{2,0,1:T(8,128)(2,1)} %param.13) | data formatting | bytes 294912 | tf_op args[0]
  4.4 1.7 %copy.20.cot = bf16[64,9,128]{2,1,0:T(8,128)(2,1)} copy(bf16[64,9,128]{2,0,1:T(8,128)(2,1)} %param.14) | data formatting | bytes 294912 | tf_op args[1]
  6.2 5.3 %shard_map.148 = (f32[1,128]{1,0:T(1,128)}, bf16[384,384]{1,0:T(8,128)(2,1)}, bf16[9,128,256]{2,1,0:T(8,128)(2,1)}, bf16[9,128,256]{2,1,0:T(8,128)(2,1)}) custom-call(bf16[64,9,128]{2,1,0:T(8,128)(2,1)} %copy.19.feats, bf16[64,9,128]{2,1,0:T(8,128)(2,1)} %copy.20.cot, bf16[9,9,256]{2,1,0:T(8,128)(2,1)} %frames.3, bf16[256,128]{1,0:T(8,128)(2,1)} %radial.3, ...), custom_call_target="tpu_custom_call" | custom-call | tf_op jit(solution)/shard_map/pallas_call | solution.py:335
  11.5 35.8 %shard_map.149 = (f32[8,4,1,128]{3,2,1,0:T(1,128)}, bf16[8,4,96,384]{3,2,1,0:T(8,128)(2,1)}, bf16[384,384]{1,0:T(8,128)(2,1)}) custom-call(f32[1,128]{1,0:T(1,128)} %get-tuple-element.12.mix, bf16[384,384]{1,0:T(8,128)(2,1)} %get-tuple-element.13.weight_grad, bf16[28,96,384]{2,1,0:T(8,128)(2,1)} %experts.1), custom_call_target="tpu_custom_call" | custom-call | tf_op jit(solution)/shard_map/pallas_call | solution.py:350
  47.3 9.5 %shard_map.150 = (bf16[64,9,128]{2,1,0:T(8,128)(2,1)}, f32[64,9,128]{2,1,0:T(8,128)}, f32[28,96,384]{2,1,0:T(8,128)}) custom-call(bf16[64,9,128]{2,1,0:T(8,128)(2,1)} %copy.19.feats, bf16[64,9,128]{2,1,0:T(8,128)(2,1)} %copy.20.cot, bf16[9,9,256]{2,1,0:T(8,128)(2,1)} %frames.3, bf16[256,128]{1,0:T(8,128)(2,1)} %radial.3, s32[1,256]{1,0:T(1,128)} %bitcast.11, ...), custom_call_target="tpu_custom_call" | custom-call | tf_op jit(solution)/shard_map/pallas_call | solution.py:368
  56.8 1.7 %copy.21 = bf16[64,9,128]{2,0,1:T(8,128)(2,1)} copy(bf16[64,9,128]{2,1,0:T(8,128)(2,1)} %get-tuple-element.17) | data formatting | bytes 294912 | tf_op jit(solution)/shard_map/pallas_call | solution.py:368
  58.4 1.9 %copy.22 = f32[64,9,128]{2,0,1:T(8,128)} copy(f32[64,9,128]{2,1,0:T(8,128)} %get-tuple-element.18) | data formatting | bytes 589824 | tf_op jit(solution)/shard_map/pallas_call | solution.py:368

commit v2 on v1

--- a/solution.py
+++ b/solution.py
@@ -71,11 +71,11 @@
 
 def before_kernel(
     feats, cot, frames, radial, source, target, valid, types, dataset, type_table, dataset_table, router,
-    mix, weight_grad, rotated, dcomb, spread_scr, gat_scr, dun_scr, frame_scr, rad_scr, router_scr,
+    mix, weight_grad, rotated, dcomb, gat_scr, dun_scr, frame_scr, rad_scr, router_scr,
 ):
-    atoms, comps, channels = feats.shape
+    comps, atoms, channels = feats.shape
     zero_rows = [d * d + d for d in range(math.isqrt(comps))]
-    n_types, n_exp = type_table.shape[0], router.shape[1]
+    n_types, n_exp = type_table.shape[0], router.shape[0]
     onehot = (lax.broadcasted_iota(jnp.int32, (n_types, atoms), 0) == types[...]).astype(F32)
     counts = jnp.sum(onehot, axis=1, keepdims=True)
     embed = jnp.sum(counts * type_table[...], axis=0, keepdims=True) / atoms
@@ -83,8 +83,8 @@
     pick = (lax.broadcasted_iota(jnp.int32, (n_sets, 1), 0) == dataset[...]).astype(F32)
     embed = embed + jnp.sum(pick * dataset_table[...], axis=0, keepdims=True)
     router_scr[...] = jnp.zeros_like(router_scr)
-    router_scr[:, :n_exp] = router[...]
-    logits = lax.dot_general(embed, router_scr[...], NN, precision=lax.Precision.HIGHEST, preferred_element_type=F32)
+    router_scr[:n_exp, :] = router[...]
+    logits = lax.dot_general(embed, router_scr[...], NT, precision=lax.Precision.HIGHEST, preferred_element_type=F32)
     soft = jnp.maximum(logits, 0.0) + jnp.log1p(jnp.exp(-jnp.abs(logits)))
     soft = jnp.where(lax.broadcasted_iota(jnp.int32, soft.shape, 1) < n_exp, soft, 0.0)
     mix[...] = soft / jnp.sum(soft, axis=1, keepdims=True)
@@ -94,12 +94,9 @@
     src = hits(source[...], atoms).astype(BF16)
     tgt = (hits(target[...], atoms) & (valid[...] > 0)).astype(BF16)
     scale = atoms / source.shape[1]
-    spread_scr[...] = feats[...].astype(F32)
     for j in range(comps):
-        gat_scr[j] = dot(spread_scr[:, j, :].astype(BF16), src, TN).astype(BF16)
-    spread_scr[...] = cot[...].astype(F32) * scale
-    for j in range(comps):
-        dun_scr[j] = dot(spread_scr[:, j, :].astype(BF16), tgt, TN).astype(BF16)
+        gat_scr[j] = dot(feats[j], src, TN).astype(BF16)
+        dun_scr[j] = (dot(cot[j], tgt, TN) * scale).astype(BF16)
 
     def out(i, at, a, b):
         rotated[i, at, :] = a.astype(BF16)
@@ -120,7 +117,11 @@
 ):
     z, r = lax.axis_index("shard"), lax.axis_index("replica")
     n_exp, block, width = experts.shape
-    peers = [lax.rem(z + o, group) for o in range(group)]
+    offsets = sorted(range(group), key=lambda o: min(o, group - o))
+    peers = [lax.rem(z + o, group) for o in offsets]
+    owners = [lax.rem(z + group - o, group) for o in offsets]
+    parts = 2 if block % (2 * ROWS) == 0 else 1
+    depth = block // parts
     core = lax.rem(r, 2)
     bits = max(replicas.bit_length() - 1, 1)
     dims = [1 << b for b in range(1, bits)]
@@ -158,10 +159,12 @@
         copy.start()
     wg_copies = [
         remote(
-            weight_grad.at[pl.ds(pl.multiple_of(p * block, ROWS), block)],
-            rows_all.at[r, z], wg_send.at[n], rows_recv.at[r, z], (p, r),
+            weight_grad.at[pl.ds(pl.multiple_of(p * block + q * depth, ROWS), depth)],
+            rows_all.at[r, z, pl.ds(q * depth, depth)],
+            wg_send.at[n * parts + q], rows_recv.at[r, z * parts + q], (p, r),
         )
         for n, p in enumerate(peers[1:])
+        for q in range(parts)
     ]
     for copy in wg_copies:
         copy.start()
@@ -169,68 +172,84 @@
     sent = [0]
     pending = []
 
-    def forward(n, mask):
+    def slot_of(who, item):
+        owner, q = owners[item // parts], item % parts
+        return rows_all.at[who, owner, pl.ds(q * depth, depth)], rows_recv.at[who, owner * parts + q]
+
+    def forward(item, mask):
         who = r
         top = -1
         for k in range(len(dims)):
             if mask >> k & 1:
                 who = flip(who, order[k])
                 top = k
-        slot = rows_all.at[who, peers[n]]
-        if mask or n:
-            remote(slot, slot, own_send.at[0], rows_recv.at[who, peers[n]], (z, r)).wait_recv()
+        slot, arrived = slot_of(who, item)
+        if mask or item >= parts:
+            remote(slot, slot, own_send.at[0], arrived, (z, r)).wait_recv()
         goals = [flip(r, order[k]) for k in range(top + 1, len(dims))] + [sibling]
         for goal in goals if replicas > 1 else []:
-            copy = remote(slot, slot, own_send.at[sent[0]], rows_recv.at[who, peers[n]], (z, goal))
+            copy = remote(slot, slot, own_send.at[sent[0]], arrived, (z, goal))
             copy.start()
             pending.append(copy)
             sent[0] += 1
 
+    masks = 1 << len(dims)
     keep.wait()
-    forward(0, 0)
-
-    for n, p in enumerate(peers[1:]):
-        remote(mix, mix_group.at[p], mix_send.at[0], mix_recv.at[p], (z, r)).wait_recv()
+    for item in range(parts):
+        forward(item, 0)
+
     mixall_copies = []
-    for o in range(1, replicas):
-        copy = remote(
-            mix_group, mix_all.at[r], mixall_send.at[o - 1], mixall_recv.at[r], (z, lax.rem(r + o, replicas))
-        )
-        copy.start()
-        mixall_copies.append(copy)
-    mix_all[r] = mix_group[...]
-    kron_scr[...] = spread(mix_group[...].reshape(group, mix.shape[1]), group, n_exp, False)
-    fetch.wait()
-    for t in range(block // ROWS):
+    merged_copies = []
+    own_rows = pl.ds(pl.multiple_of(z * block, ROWS), block)
+    tiles = block // ROWS
+
+    def mixtures():
+        for p in owners[1:]:
+            remote(mix, mix_group.at[p], mix_send.at[0], mix_recv.at[p], (z, r)).wait_recv()
+        for o in range(1, replicas):
+            copy = remote(
+                mix_group, mix_all.at[r], mixall_send.at[o - 1], mixall_recv.at[r], (z, lax.rem(r + o, replicas))
+            )
+            copy.start()
+            mixall_copies.append(copy)
+        mix_all[r] = mix_group[...]
+        kron_scr[...] = spread(mix_group[...].reshape(group, mix.shape[1]), group, n_exp, False)
+        fetch.wait()
+
+    def merge(t):
         at = slice(t * ROWS, (t + 1) * ROWS)
-        shares[:, at, :] = (
-            dot(kron_scr[...], experts_scr[:, at, :].reshape(n_exp * ROWS, width)).astype(BF16).reshape(group, ROWS, width)
-        )
-    own_rows = pl.ds(pl.multiple_of(z * block, ROWS), block)
-    merged_copies = [
-        remote(shares.at[p], merged.at[own_rows], merged_send.at[n], merged_recv.at[z], (p, r))
-        for n, p in enumerate(peers[1:])
-    ]
-    for copy in merged_copies:
-        copy.start()
-    merged[own_rows, :] = shares[z]
-
-    masks = 1 << len(dims)
-    for n in range(1, group):
-        forward(n, 0)
+        rows = dot(kron_scr[...], experts_scr[:, at, :].reshape(n_exp * ROWS, width))
+        shares[:, at, :] = rows.astype(BF16).reshape(group, ROWS, width)
+
+    def send_merged():
+        for n, p in enumerate(peers[1:]):
+            merged_copies.append(
+                remote(shares.at[p], merged.at[own_rows], merged_send.at[n], merged_recv.at[z], (p, r))
+            )
+            merged_copies[-1].start()
+        merged[own_rows, :] = shares[z]
+
+    todo = [mixtures] + [functools.partial(merge, t) for t in range(tiles)] + [send_merged]
+    items = group * parts
+    for item in range(parts, items + parts):
+        if item < items:
+            forward(item, 0)
         for mask in range(1, masks):
-            forward(n - 1, mask)
-    for mask in range(1, masks):
-        forward(group - 1, mask)
+            forward(item - parts, mask)
+        for job in todo[:3]:
+            job()
+        todo = todo[3:]
+    for job in todo:
+        job()
     if replicas > 1:
-        for n in range(group):
+        for item in range(items):
             for mask in range(masks):
                 who = sibling
                 for k in range(len(dims)):
                     if mask >> k & 1:
                         who = flip(who, dims[k])
-                slot = rows_all.at[who, peers[n]]
-                remote(slot, slot, own_send.at[0], rows_recv.at[who, peers[n]], (z, r)).wait_recv()
+                slot, arrived = slot_of(who, item)
+                remote(slot, slot, own_send.at[0], arrived, (z, r)).wait_recv()
     for o in range(1, replicas):
         who = lax.rem(r + o, replicas)
         remote(mix_group, mix_all.at[who], mixall_send.at[0], mixall_recv.at[who], (z, r)).wait_recv()
@@ -244,9 +263,9 @@
 def after_kernel(
     feats, cot, frames, radial, source, target, valid, rotated, dcomb, merged, mix_all, rows_all,
     updated, feats_grad, expert_grad,
-    spread_scr, msg_scr, drot_scr, un_scr, dgat_scr, frame_scr, rad_scr, kron_scr, out_scr, out_sem,
+    msg_scr, drot_scr, un_scr, dgat_scr, frame_scr, rad_scr, kron_scr, out_scr, out_sem,
 ):
-    atoms, comps, channels = feats.shape
+    comps, atoms, channels = feats.shape
     zero_rows = [d * d + d for d in range(math.isqrt(comps))]
     systems, block, width = rows_all.shape
     n_exp = expert_grad.shape[0]
@@ -296,10 +315,8 @@
     tgt = (hits(target[...], atoms) & (valid[...] > 0)).astype(BF16)
     scale = atoms / source.shape[1]
     for i in range(comps):
-        spread_scr[:, i, :] = dot(tgt, un_scr[i], NT) * scale
-        feats_grad[:, i, :] = dot(src, dgat_scr[i], NT).astype(BF16).astype(F32)
-    updated[...] = (feats[...].astype(F32) + spread_scr[...]).astype(BF16)
-    feats_grad[...] = feats_grad[...] + cot[...].astype(F32)
+        updated[i] = (feats[i].astype(F32) + dot(tgt, un_scr[i], NT) * scale).astype(BF16)
+        feats_grad[i] = cot[i].astype(F32) + dot(src, dgat_scr[i], NT).astype(BF16).astype(F32)
     for copy in copies[-2:]:
         copy.wait()
 
@@ -326,6 +343,7 @@
     atoms, comps, channels = atom_feats.shape
     edges = edge_source.shape[0]
     n_exp, block, width = experts.shape
+    feats, cot = atom_feats.transpose(1, 0, 2), cotangent.transpose(1, 0, 2)
     source, target, valid = (a.reshape(1, edges) for a in (edge_source, edge_target, edge_valid))
     shape = jax.ShapeDtypeStruct
     stack = (comps, channels, edges)
@@ -336,16 +354,16 @@
         before_kernel,
         [shape((1, lanes), F32), shape((block * group, width), BF16), shape(stack, BF16), shape(stack, BF16)],
         [
-            VMEM((atoms, comps, channels), F32), VMEM(stack, BF16), VMEM(stack, BF16), frame_scr, rad_scr,
-            VMEM((router_weight.shape[0], lanes), F32),
+            VMEM(stack, BF16), VMEM(stack, BF16), frame_scr, rad_scr, VMEM((lanes, router_weight.shape[0]), F32),
         ],
         [0] * 12,
     )(
-        atom_feats, cotangent, frames, radial, source, target, valid, atom_types.reshape(1, atoms),
-        dataset.reshape(1, 1), type_table, dataset_table, router_weight,
+        feats, cot, frames, radial, source, target, valid, atom_types.reshape(1, atoms),
+        dataset.reshape(1, 1), type_table, dataset_table, router_weight.T,
     )
     sem = pltpu.SemaphoreType.DMA
     few = max(group - 1, 1)
+    parts = 2 if block % (2 * ROWS) == 0 else 1
     many = max(replicas - 1, 1)
     mix_all, rows_all, merged = call(
         functools.partial(exchange_kernel, group, replicas),
@@ -357,8 +375,8 @@
         [
             VMEM((group, 1, lanes), F32), VMEM((group, block, width), BF16), VMEM(experts.shape, BF16),
             VMEM((group * ROWS, n_exp * ROWS), BF16),
-            sem((2,)), sem((few,)), sem((group,)), sem((many,)), sem((replicas,)), sem((few,)),
-            sem((many * group,)), sem((replicas, group)), sem((few,)), sem((group,)),
+            sem((2,)), sem((few,)), sem((group,)), sem((many,)), sem((replicas,)), sem((few * parts,)),
+            sem((many * group * parts,)), sem((replicas, group * parts)), sem((few,)), sem((group,)),
         ],
         [0, 0, 1],
         collective=0,
@@ -367,19 +385,18 @@
     piece = min(systems, 32)
     updated, feats_grad, expert_grad = call(
         after_kernel,
-        [shape(atom_feats.shape, BF16), shape(atom_feats.shape, F32), shape(experts.shape, F32)],
+        [shape(feats.shape, BF16), shape(feats.shape, F32), shape(experts.shape, F32)],
         [
-            VMEM((atoms, comps, channels), F32), VMEM(stack, BF16), VMEM(stack, BF16), VMEM(stack, BF16),
-            VMEM(stack, BF16), frame_scr, rad_scr, VMEM((systems // piece, n_exp * ROWS, piece * ROWS), BF16),
+            VMEM(stack, BF16), VMEM(stack, BF16), VMEM(stack, BF16), VMEM(stack, BF16), frame_scr, rad_scr, VMEM((systems // piece, n_exp * ROWS, piece * ROWS), BF16),
             VMEM((2, n_exp, ROWS, width), F32), sem((2,)),
         ],
         [0] * 12,
         [0, 0, 1],
     )(
-        atom_feats, cotangent, frames, radial, source, target, valid, rotated, dcomb, merged,
+        feats, cot, frames, radial, source, target, valid, rotated, dcomb, merged,
         mix_all.reshape(systems, 1, lanes), rows_all.reshape(systems, block, width),
     )
-    return (updated, feats_grad, expert_grad)
+    return (updated.transpose(1, 0, 2), feats_grad.transpose(1, 0, 2), expert_grad)
 
 
 def solution(mesh):

time: 60.6 us -> 57.7 us (0.952)
  the two profiles are of different devices: /device:TPU:9 before, /device:TPU:0 now
where the time goes in v2:
time: 57.7 us; the launch traced here: 57.5 us
  Pallas kernels  56.2 us (97%)
  between operations  1.29 us (2%)
    pallas_call x1, Pallas kernels, shards(): call(functools.partial(exchange_kernel, group, replicas), [shape((replica...  42.3 us
    pallas_call x1, Pallas kernels, shards(): call(after_kernel, [shape(feats.shape, BF16), shape(feats.shape, F32), sh...  9.08 us
    pallas_call x1, Pallas kernels, shards(): call(before_kernel, [shape((1, lanes), F32), shape((block * group, width)...  4.9 us

profile of v2, /device:TPU:0, one launch (start us, length us, event | category | flops | bytes accessed | tf_op | source)
XLA Modules:
  0.0 57.5 jit_solution(14437537350777251756)
XLA Ops:
  1.3 4.9 %shard_map.148 = (f32[1,128]{1,0:T(1,128)}, bf16[384,384]{1,0:T(8,128)(2,1)}, bf16[9,128,256]{2,1,0:T(8,128)(2,1)}, bf16[9,128,256]{2,1,0:T(8,128)(2,1)}) custom-call(bf16[9,64,128]{2,1,0:T(8,128)(2,1)} %bitcast.14, bf16[9,64,128]{2,1,0:T(8,128)(2,1)} %bitcast.16, bf16[9,9,256]{2,1,0:T(8,128)(2,1)} %frames.3, bf16[256,128]{1,0:T(8,128)(2,1)} %radial.3, ...), custom_call_target="tpu_custom_call" | custom-call | tf_op jit(solution)/shard_map/pallas_call | solution.py:353
  6.2 42.3 %shard_map.149 = (f32[8,4,1,128]{3,2,1,0:T(1,128)}, bf16[8,4,96,384]{3,2,1,0:T(8,128)(2,1)}, bf16[384,384]{1,0:T(8,128)(2,1)}) custom-call(f32[1,128]{1,0:T(1,128)} %get-tuple-element.15.mix, bf16[384,384]{1,0:T(8,128)(2,1)} %get-tuple-element.16.weight_grad, bf16[28,96,384]{2,1,0:T(8,128)(2,1)} %experts.1), custom_call_target="tpu_custom_call" | custom-call | tf_op jit(solution)/shard_map/pallas_call | solution.py:368
  48.4 9.1 %shard_map.150 = (bf16[9,64,128]{2,1,0:T(8,128)(2,1)}, f32[9,64,128]{2,1,0:T(8,128)}, f32[28,96,384]{2,1,0:T(8,128)}) custom-call(bf16[9,64,128]{2,1,0:T(8,128)(2,1)} %bitcast.15, bf16[9,64,128]{2,1,0:T(8,128)(2,1)} %bitcast.17, bf16[9,9,256]{2,1,0:T(8,128)(2,1)} %frames.3, bf16[256,128]{1,0:T(8,128)(2,1)} %radial.3, s32[1,256]{1,0:T(1,128)} %bitcast.21, ...), custom_call_target="tpu_custom_call" | custom-call | tf_op jit(solution)/shard_map/pallas_call | solution.py:386
